TPU v7x, 128 devices: a whole 4x4x4 slice. The times are simulated.
128 devices in a mesh: batch: 8 (over x, core), seq: 16 (over z, y).
Axes of the slice: x: 4, y: 4, z: 4, core: 2. Of those that a mesh axis runs over, the one named last changes fastest.
Arguments:
- query: bfloat16 [16, 64, 128], P('batch'), may hold values from -300 to 300
- cache_keys: bfloat16 [16, 32768, 512], P('batch', 'seq'), may hold values from -6 to 6
- cache_values: bfloat16 [16, 32768, 512], P('batch', 'seq'), may hold values from -6 to 6
- new_keys: bfloat16 [16, 512], P('batch'), may hold values from -6 to 6
- new_values: bfloat16 [16, 512], P('batch'), may hold values from -6 to 6
- key_up: bfloat16 [512, 1024], P('seq'), may hold values from -0.25 to 0.25
- value_up: bfloat16 [512, 1024], P('seq'), may hold values from -0.25 to 0.25
- out_weight: bfloat16 [8192, 8192], P('seq', 'batch'), may hold values from -0.5 to 0.5
- lengths: int32 [16], P('batch'), may hold values from 128 to 32768, as said below
Outputs:
- mixed: bfloat16 [16, 8192], P('seq', 'batch')
Inputs may be any that keep to these rules, and one draw needn't show every extreme that they name: `lengths`: every length is a multiple of 128, at least 128; some sequence fills all 32768 slots. Slots at or beyond a sequence's length hold arbitrary finite entries that must not affect the result.
All inputs are finite; a program needn't handle non-finite values.
Results may differ from a plain program's by a relative error of at most 0.019.
Values may be sent and summed in bfloat16 or wider, within the bound.
No kernel may reach another device: no remote copies, remote signals or barrier semaphores. Data moves between devices by JAX's collectives and lax.ppermute only.
A program may use at most 64 MiB of HBM per device.

v0:
```python
import jax
import jax.numpy as jnp
from jax import lax
from jax.sharding import Mesh
from jax.sharding import PartitionSpec as P

SEQ = ("seq_0", "seq_1")


NEGATIVE = -1e30
TOP_PRECISION = lax.Precision.HIGHEST


def in_order(pieces, dim):
    shape = list(pieces.shape[1:])
    shape[dim] *= pieces.shape[0]
    return jnp.moveaxis(pieces, 0, dim).reshape(shape)


def from_everyone(value, axis):
    size = lax.axis_size(axis)
    return lax.all_to_all(
        jnp.broadcast_to(value[None], (size, *value.shape)), axis, 0, 0, tiled=True
    )


def collect(value, axis, dim):
    return in_order(from_everyone(value, axis), dim)


def all_in_one(value, axis):
    leaves = jax.tree.leaves(value)
    order = sorted(range(len(leaves)), key=lambda k: -leaves[k].size)
    width = (1, *leaves[order[0]].shape)[-1]
    lines = [
        jnp.pad(leaves[k].reshape(-1), (0, -leaves[k].size % width)).reshape(-1, width)
        for k in order
    ]
    both, at, found = (lax.all_gather(jnp.concatenate(lines), axis), 0, {})
    for k, line in zip(order, lines):
        piece = both[:, at : at + len(line)].reshape(len(both), -1)
        found[k] = piece[:, : leaves[k].size].reshape(-1, *leaves[k].shape)
        at += len(line)
    numbers = iter(range(len(leaves)))
    return jax.tree.map(lambda _: found[next(numbers)], value)


def merged_by_axis(value, axes, combine):
    for axis in axes:
        pieces = all_in_one(value, axis)
        value = jax.tree.map(lambda part: part[0], pieces)
        for k in range(1, lax.axis_size(axis)):
            value = combine(value, jax.tree.map(lambda part: part[k], pieces))
    return value


def in_blocks(value, dim, size):
    shape = value.shape
    pieces = value.reshape(*shape[:dim], size, shape[dim] // size, *shape[dim + 1 :])
    return jnp.moveaxis(pieces, dim, 0)


def sent_and_summed(value, axis, dim):
    size = lax.axis_size(axis)
    pieces = lax.all_to_all(in_blocks(value, dim, size), axis, 0, 0, tiled=True)
    return jnp.sum(pieces.astype(jnp.float32), axis=0)


def combine_parts(first, second):
    first_max, first_sum, first_totals = first
    second_max, second_sum, second_totals = second
    upper_limit = jnp.maximum(first_max, second_max)
    first_scale = jnp.exp(first_max - upper_limit)
    second_scale = jnp.exp(second_max - upper_limit)
    return (
        upper_limit,
        first_sum * first_scale + second_sum * second_scale,
        first_totals * first_scale[..., None] + second_totals * second_scale[..., None],
    )


def body(
    query, cache_keys, cache_values, new_keys, new_values, key_up, value_up, out_weight, lengths
):
    batch_rows, cache_len, rank_full = cache_keys.shape
    head_count, head_dimension = (query.shape[1], query.shape[2])
    kv_heads = key_up.shape[1] // head_dimension
    group_size = head_count // kv_heads
    score_scale_factor = head_dimension ** (-0.5)
    seq_index = lax.axis_index(SEQ)
    seq_count = lax.axis_size(SEQ)
    local_head_index = head_count // seq_count
    positions = seq_index * cache_len + lax.iota(jnp.int32, cache_len)
    live_mask = (positions[None, :] < lengths[:, None])[:, None, None, :]
    grouped = query.reshape(batch_rows, kv_heads, group_size, head_dimension)
    local_rank = key_up.shape[0]
    query_part = jnp.einsum(
        "bkgd,rkd->bkgr",
        grouped,
        key_up.reshape(local_rank, kv_heads, head_dimension),
        preferred_element_type=jnp.float32,
    )
    query_latent = collect(query_part, SEQ, 3)
    value_full = collect(value_up, SEQ, 0)
    scores = (
        jnp.einsum(
            "bkgr,blr->bkgl",
            query_latent,
            cache_keys,
            precision=TOP_PRECISION,
            preferred_element_type=jnp.float32,
        )
        * score_scale_factor
    )
    current_token_score = (
        jnp.einsum(
            "bkgr,br->bkg", query_latent, new_keys.astype(jnp.float32), precision=TOP_PRECISION
        )
        * score_scale_factor
    )
    value_table = value_full.astype(jnp.float32).reshape(rank_full, kv_heads, head_dimension)
    new_value = jnp.dot(new_values, value_full, preferred_element_type=jnp.float32).reshape(
        batch_rows, kv_heads, head_dimension
    )
    scores = jnp.where(live_mask, scores, NEGATIVE)
    local_max = jnp.max(scores, axis=-1)
    softmax_terms = jnp.where(live_mask, jnp.exp(scores - local_max[..., None]), 0.0)
    denominator = jnp.sum(softmax_terms, axis=-1)
    latent_sum = jnp.einsum(
        "bkgl,blr->bkgr",
        softmax_terms,
        cache_values,
        precision=TOP_PRECISION,
        preferred_element_type=jnp.float32,
    )
    totals = jnp.einsum("bkgr,rkd->bkgd", latent_sum, value_table, precision=TOP_PRECISION)
    merged_max, denominator, totals = merged_by_axis(
        (local_max, denominator, totals), SEQ, combine_parts
    )
    upper_limit = jnp.maximum(merged_max, current_token_score)
    rescale = jnp.exp(merged_max - upper_limit)
    finish_denominator = denominator * rescale
    finish_totals = totals * rescale[..., None]
    own_weight = jnp.exp(current_token_score - upper_limit)
    normalized = (finish_totals + own_weight[..., None] * new_value[:, :, None, :]) / (
        finish_denominator + own_weight
    )[..., None]
    normalized = normalized.reshape(batch_rows, head_count * head_dimension)
    width_local = local_head_index * head_dimension
    attended = lax.dynamic_slice_in_dim(normalized, seq_index * width_local, width_local, 1).astype(
        jnp.bfloat16
    )
    partial_out = jnp.dot(
        collect(attended, "batch", 0), out_weight, preferred_element_type=jnp.float32
    )
    return sent_and_summed(partial_out.astype(jnp.bfloat16), SEQ, 0).astype(jnp.bfloat16)


def solution(mesh):
    torus = Mesh(mesh.devices.reshape(mesh.shape["batch"], 4, 4), ("batch", "seq_0", "seq_1"))
    return jax.shard_map(
        body,
        mesh=torus,
        in_specs=(
            P("batch", None, None),
            P("batch", SEQ, None),
            P("batch", SEQ, None),
            P("batch", None),
            P("batch", None),
            P(SEQ, None),
            P(SEQ, None),
            P(SEQ, "batch"),
            P("batch"),
        ),
        out_specs=P(SEQ, "batch"),
        check_vma=False,
    )
```

profile of v0, /device:TPU:0, one launch (start us, length us, event | category | flops | bytes accessed | tf_op | source)
XLA Modules:
  0.0 103.4 jit_solution(17169264877539811259)
XLA Ops:
  0.0 0.9 copy.41
  0.9 0.9 convolution_bitcast_fusion.1
  2.0 1.1 %reshape.574 = f32[16,1,4096]{2,1,0:T(1,128)} reshape(f32[16,2,8,8,32]{4,3,2,1,0:T(8,128)S(1)} %broadcast_in_dim.25) | data formatting | bytes 524288
  3.1 8.2 %all-to-all-start = ((f32[16,1,4096]{2,1,0:T(1,128)}), f32[16,1,4096]{2,1,0:T(1,128)S(1)}, u32[]{:S(2)}, u32[]{:S(2)}) async-start(f32[16,1,4096]{2,1,0:T(1,128)} %reshape.574), calls=%async_computation | async-start | bytes 524288 | tf_op jit(solution)/shard_map/all_to_all | solution.py:22
  11.3 0.7 broadcast_compare_fusion
  12.1 7.9 %all-to-all-done = f32[16,1,4096]{2,1,0:T(1,128)S(1)} async-done(((f32[16,1,4096]{2,1,0:T(1,128)}), f32[16,1,4096]{2,1,0:T(1,128)S(1)}, u32[]{:S(2)}, u32[]{:S(2)}) %all-to-all-start) | async-done | bytes 262176 | tf_op jit(solution)/shard_map/all_to_all | solution.py:22
  20.0 2.0 %broadcast_in_dim.28 = bf16[16,32,1024]{2,1,0:T(8,128)(2,1)} broadcast(bf16[32,1024]{1,0:T(8,128)(2,1)} %param.15), dimensions={1,2} | broadcast | bytes 1114112 | tf_op jit(solution)/shard_map/broadcast_in_dim | solution.py:23
  21.9 3.7 %all-to-all-start.1 = ((bf16[16,32,1024]{2,1,0:T(8,128)(2,1)}), bf16[16,32,1024]{2,1,0:T(8,128)(2,1)S(1)}, u32[]{:S(2)}, u32[]{:S(2)}) async-start(bf16[16,32,1024]{2,1,0:T(8,128)(2,1)} %broadcast_in_dim.28), calls=%async_computation.1 | async-start | bytes 2097152 | tf_op jit(solution)/shard_map/all_to_all | solution.py:22
  26.1 1.3 %reduce.34 = f32[16,4096]{1,0:T(8,128)S(1)} reduce(f32[16,1,4096]{2,1,0:T(1,128)S(1)} %all-to-all-done, f32[]{:T(128)} %broadcast.67), dimensions={1}, to_apply=%all_to_all.12.reduce_sub_computation | reduce | bytes 524292 | tf_op jit(solution)/shard_map/all_to_all | solution.py:22
  27.7 1.7 %copy.25 = f32[2,8,8,16,32]{4,3,2,1,0:T(8,128)} copy(f32[2,8,8,16,32]{4,2,1,0,3:T(8,128)S(1)} %bitcast.259) | data formatting | bytes 524288 | tf_op jit(solution)/shard_map/transpose | solution.py:17
  29.4 1.6 %reshape.508 = f32[2,8,8,512]{3,2,1,0:T(8,128)S(1)} reshape(f32[2,8,8,16,32]{4,3,2,1,0:T(8,128)} %copy.25) | data formatting | bytes 524288 | tf_op jit(solution)/shard_map/reshape | solution.py:17
  31.0 6.2 %fusion.55 = (f32[2,8,8]{2,1,0:T(8,128)S(1)}, f32[2,8,8,2048]{3,2,1,0:T(8,128)S(1)}) fusion(f32[2,8,8,512]{3,2,1,0:T(8,128)S(1)} %reshape.508, bf16[2,2048,512]{2,1,0:T(8,128)(2,1)} %param.10, pred[2,2048]{1,0:T(4,128)(4,1)S(1)} %broadcast_compare_fusion), kind=kOutput, calls=%fused_computation.122 | convolution fusion | flops 1611399040 | bytes 5509632 | tf_op jit(solution)/shard_map/bkgr,blr->bkgl/dot_general | solution.py:106
  37.3 1.3 %fusion.53 = (f32[2,8,8]{2,1,0:T(8,128)S(1)}, f32[2,8,8,2048]{3,2,1,0:T(8,128)}) fusion(f32[2,8,8,2048]{3,2,1,0:T(8,128)S(1)} %get-tuple-element.38, f32[2,8,8]{2,1,0:T(8,128)S(1)} %get-tuple-element.37, pred[2,2048]{1,0:T(4,128)(4,1)S(1)} %broadcast_compare_fusion), kind=kLoop, calls=%fused_computation.120 | loop fusion | flops 786304 | bytes 2102272 | tf_op jit(solution)/shard_map/reduce_sum | solution.py:128
  38.7 1.0 fusion.28
  39.6 4.8 %fusion.2 = f32[2,8,8,512]{3,2,0,1:T(8,128)S(1)} fusion(bf16[2,2048,512]{2,1,0:T(8,128)(2,1)} %param.11, f32[2,8,8,2048]{3,2,1,0:T(8,128)} %get-tuple-element.27), kind=kOutput, calls=%fused_computation.2 | convolution fusion | flops 1610612736 | bytes 5505024 | tf_op jit(solution)/shard_map/bkgl,blr->bkgr/dot_general | solution.py:129
  45.3 13.1 %all-gather.2 = f32[4,130,128]{2,1,0:T(8,128)S(1)} all-gather(f32[1,130,128]{2,1,0:T(8,128)S(1)} %maximum_bitcast_fusion), channel_id=2, replica_groups=mesh['batch'=8,'seq_0'=4,'seq_1'=4] {'seq_0'}, dimensions={0}, use_global_device_ids=true | all-gather | bytes 332800 | tf_op jit(solution)/shard_map/all_gather | solution.py:39
  58.7 12.6 %all-gather.3 = f32[4,130,128]{2,1,0:T(8,128)S(1)} all-gather(f32[1,130,128]{2,1,0:T(8,128)S(1)} %maximum_bitcast_fusion.1), channel_id=3, replica_groups=mesh['batch'=8,'seq_0'=4,'seq_1'=4] {'seq_1'}, dimensions={0}, use_global_device_ids=true | all-gather | bytes 332800 | tf_op jit(solution)/shard_map/all_gather | solution.py:39
  73.0 0.7 copy.75
  73.8 0.7 copy.73
  75.7 1.1 %fusion.31 = f32[2,8,128]{2,0,1:T(2,128)S(1)} fusion(bf16[8,128,512]{2,1,0:T(8,128)(2,1)S(1)} %bitcast.261, bf16[2,512]{1,0:T(2,128)(2,1)} %param.13), kind=kOutput, calls=%fused_computation.73 | convolution fusion | flops 2097152 | bytes 1058816 | tf_op jit(solution)/shard_map/dot_general | solution.py:122
  76.7 0.8 multiply_bitcast_fusion
  78.0 0.7 fusion.30
  78.8 9.5 %all_to_all.20 = bf16[8,2,512]{2,1,0:T(2,128)(2,1)S(1)} all-to-all(bf16[8,2,512]{2,1,0:T(2,128)(2,1)S(1)} %broadcast_in_dim.29), channel_id=1, replica_groups=mesh['batch'=8,'seq_0'=4,'seq_1'=4] {'batch'}, dimensions={0} | all-to-all | bytes 32768 | tf_op jit(solution)/shard_map/all_to_all | solution.py:22
  89.7 13.0 %all_to_all.21 = bf16[16,2,512]{2,1,0:T(2,128)(2,1)S(1)} all-to-all(bf16[16,2,512]{2,1,0:T(2,128)(2,1)S(1)} %reshape.576), channel_id=1, replica_groups=mesh['batch'=8,'seq_0'=4,'seq_1'=4] {'seq_0','seq_1'}, dimensions={0} | all-to-all | bytes 65536 | tf_op jit(solution)/shard_map/all_to_all | solution.py:65
  (56 shorter events, 7.8 us)
Async XLA Ops:
  0.0 88.2 %copy-start = (bf16[512,1024]{1,0:T(8,128)(2,1)S(1)}, bf16[512,1024]{1,0:T(8,128)(2,1)}, u32[]{:S(2)}) copy-start(bf16[512,1024]{1,0:T(8,128)(2,1)} %param.16) | copy-start | bytes 3145732
  3.1 16.9 %all-to-all-start = ((f32[16,1,4096]{2,1,0:T(1,128)}), f32[16,1,4096]{2,1,0:T(1,128)S(1)}, u32[]{:S(2)}, u32[]{:S(2)}) async-start(f32[16,1,4096]{2,1,0:T(1,128)} %reshape.574), calls=%async_computation | async-start | bytes 524288 | tf_op jit(solution)/shard_map/all_to_all | solution.py:22
  21.9 22.5 %all-to-all-start.1 = ((bf16[16,32,1024]{2,1,0:T(8,128)(2,1)}), bf16[16,32,1024]{2,1,0:T(8,128)(2,1)S(1)}, u32[]{:S(2)}, u32[]{:S(2)}) async-start(bf16[16,32,1024]{2,1,0:T(8,128)(2,1)} %broadcast_in_dim.28), calls=%async_computation.1 | async-start | bytes 2097152 | tf_op jit(solution)/shard_map/all_to_all | solution.py:22
  29.4 9.3 %copy-start.1 = (bf16[2,512]{1,0:T(2,128)(2,1)S(1)}, bf16[2,512]{1,0:T(2,128)(2,1)}, u32[]{:S(2)}) copy-start(bf16[2,512]{1,0:T(2,128)(2,1)} %param.12) | copy-start | bytes 6148
where the time goes:
time: 104 us; the launch traced here: 103 us
  blocking collectives  48.2 us (46%)
  matrix products  14.7 us (14%)
  local copies, waits for them, and re-layouts  13.8 us (13%)
  starting transfers between devices  11.8 us (11%)
  waiting for transfers between devices  7.94 us (8%)
  other arithmetic  6.65 us (6%)
    all_gather x2, blocking collectives, all_in_one(): both, at, found = (lax.all_gather(jnp.concatenate(lines), axis), 0, {})  25.7 us
    all_to_all x1, blocking collectives, sent_and_summed(): pieces = lax.all_to_all(in_blocks(value, dim, size), axis, 0, 0, tiled=True)  13 us
    all_to_all x2, starting transfers between devices, from_everyone(): lax.all_to_all(jnp.broadcast_to(value[None], (size, *value.shape)), axis,...  11.8 us
    all_to_all x1, blocking collectives, from_everyone(): lax.all_to_all(jnp.broadcast_to(value[None], (size, *value.shape)), axis,...  9.46 us
    all_to_all x2, waiting for transfers between devices, from_everyone(): lax.all_to_all(jnp.broadcast_to(value[None], (size, *value.shape)), axis,...  7.94 us
    dot_general x1, matrix products, body(): jnp.einsum('bkgr,blr->bkgl', query_latent, cache_keys, precision=TOP_PREC...  6.18 us
    unnamed x19, local copies, waits for them, and re-layouts  5.21 us
    dot_general x1, matrix products, body(): jnp.einsum('bkgl,blr->bkgr', softmax_terms, cache_values, precision=TOP_P...  4.8 us
  transfers between devices with their start and end apart: 2, of which 1 were waited for; matrix products, arithmetic and copies ran while one was open for 19% of the time, Pallas kernels for 0%

commit v1 on v0

v1 whole, which is shorter than its diff:
```python
import functools

import jax
import jax.numpy as jnp
from jax import lax
from jax.experimental import pallas as pl
from jax.experimental.pallas import tpu as pltpu
from jax.sharding import PartitionSpec as P

NEGATIVE = -1e30
FLOOR = -1e20
VMEM = pltpu.VMEM
MIB = 1024 * 1024


def iota(shape, dim):
    return lax.broadcasted_iota(jnp.int32, shape, dim)


def whole(n):
    return [pl.BlockSpec(memory_space=VMEM)] * n


def split(value):
    high = value.astype(jnp.bfloat16).astype(jnp.float32)
    return high, value - high


def latent_kernel(query_ref, key_up_ref, out_ref):
    peers, ranks, _ = out_ref.shape
    flat = query_ref[...].reshape(128, 128)
    row, col = iota((128, 128), 0), iota((128, 128), 1)
    source = ((row >> 2) & 1) * 64 + (row >> 3) * 4 + (row & 3)
    pick = jnp.where(col == source, 1.0, 0.0).astype(jnp.bfloat16)
    ordered = jnp.dot(pick, flat, preferred_element_type=jnp.float32)
    blocks = [
        jnp.where((row >> 4) == k, ordered, 0.0).astype(jnp.bfloat16) for k in range(8)
    ]
    latent = lax.dot_general(
        key_up_ref[...],
        jnp.concatenate(blocks, axis=1),
        (((1,), (1,)), ((), ())),
        preferred_element_type=jnp.float32,
    )
    high, low = split(latent)
    piece = jnp.concatenate([high, low], axis=1).astype(jnp.bfloat16)
    for k in range(peers):
        out_ref[k] = piece


def attend_kernel(
    scale,
    shift_ref,
    lengths_ref,
    latent_ref,
    keys_ref,
    values_ref,
    new_keys_ref,
    new_values_ref,
    value_up_ref,
    out_ref,
    scores_ref,
    weights_ref,
):
    peers, ranks, width = latent_ref.shape
    rank = peers * ranks
    length = keys_ref.shape[1]
    chunk = 512
    shift = shift_ref[0]
    both = latent_ref[...].reshape(rank, width)
    lane = iota((rank, width), 1)
    maps = [
        jnp.where(((lane >> 2) & 1) == b, both.astype(jnp.float32), 0.0).astype(jnp.bfloat16)
        for b in range(2)
    ]
    second = ((iota((1, 128), 1) >> 2) & 1) == 1
    limit = jnp.where(second, lengths_ref[1], lengths_ref[0]) - shift
    top = jnp.full((8, 128), FLOOR, jnp.float32)
    for c in range(length // chunk):
        at = pl.ds(c * chunk, chunk)
        raw = jnp.dot(keys_ref[0, at, :], maps[0], preferred_element_type=jnp.float32)
        raw += jnp.dot(keys_ref[1, at, :], maps[1], preferred_element_type=jnp.float32)
        scores = (raw[:, :128] + raw[:, 128:]) * scale
        live = iota((chunk, 128), 0) + c * chunk < limit
        scores = jnp.where(live, scores, NEGATIVE)
        scores_ref[at, :] = scores
        top = jnp.maximum(top, jnp.max(scores.reshape(chunk // 8, 8, 128), axis=0))
    fresh = jnp.dot(new_keys_ref[...], maps[0], preferred_element_type=jnp.float32)[0:1]
    fresh += jnp.dot(new_keys_ref[...], maps[1], preferred_element_type=jnp.float32)[1:2]
    fresh = (fresh[:, :128] + fresh[:, 128:]) * scale
    fresh = jnp.where(shift == 0, fresh, NEGATIVE)
    top = jnp.maximum(jnp.max(top, axis=0, keepdims=True), fresh)
    total = jnp.zeros((8, 128), jnp.float32)
    for c in range(length // chunk):
        at = pl.ds(c * chunk, chunk)
        weights = jnp.exp(scores_ref[at, :] - top)
        total += jnp.sum(weights.reshape(chunk // 8, 8, 128), axis=0)
        weights_ref[:, at] = weights.T.astype(jnp.bfloat16)
    own = jnp.exp(fresh - top)
    total = jnp.sum(total, axis=0, keepdims=True) + own
    top_high, rest = split(top)
    top_mid, top_low = split(rest)
    total_high, total_low = split(total)
    row = iota((128, 128), 0)
    table = jnp.zeros((128, 128), jnp.float32)
    for k, line in enumerate((top_high, top_mid, top_low, total_high, total_low, own)):
        table = jnp.where(row == k, line, table)
    table = table.T
    own_column = table[:, 5:6]
    sums = [
        jnp.dot(weights_ref[...], values_ref[b], preferred_element_type=jnp.float32)
        for b in range(2)
    ]
    fresh_values = new_values_ref[...].astype(jnp.float32)
    upper = ((iota((128, rank), 0) >> 2) & 1) == 1
    summed = jnp.where(upper, sums[1], sums[0]) + own_column * jnp.where(
        upper, fresh_values[1:2], fresh_values[0:1]
    )
    for k in range(peers):
        lines = summed[8 * k : 8 * k + 8]
        stack = [lines[:, 128 * g : 128 * g + 128] for g in range(rank // 128)]
        out_ref[k, 0:32, :] = jnp.concatenate(stack, axis=0).astype(jnp.bfloat16)
        out_ref[k, 32:64, :] = value_up_ref[:, 128 * (k // 2) : 128 * (k // 2) + 128]
        out_ref[k, 64:72, :] = table[8 * k : 8 * k + 8].astype(jnp.bfloat16)


def merge_kernel(parts_ref, out_ref):
    peers = parts_ref.shape[0]
    stats = parts_ref[:, 64:72, :].reshape(peers * 8, 128)
    row, col = iota((128, 256), 0), iota((128, 256), 1)
    pick = ((col < 128) & (row < 3)) | ((col >= 128) & ((row == 3) | (row == 4)))
    spread = jnp.dot(
        stats, jnp.where(pick, 1.0, 0.0).astype(jnp.bfloat16), preferred_element_type=jnp.float32
    )
    tops = [spread[8 * k : 8 * k + 8, :128] for k in range(peers)]
    top = functools.reduce(jnp.maximum, tops)
    total = jnp.zeros((8, 128), jnp.float32)
    sums = [jnp.zeros((8, 128), jnp.float32) for _ in range(4)]
    for k in range(peers):
        factor = jnp.exp(tops[k] - top)
        total += factor * spread[8 * k : 8 * k + 8, 128:]
        lines = parts_ref[k, 0:32, :].astype(jnp.float32)
        for g in range(4):
            sums[g] += factor * lines[8 * g : 8 * g + 8]
    latent = jnp.concatenate([s / total for s in sums], axis=1)
    high, low = split(latent)
    table = parts_ref[:, 32:64, :].reshape(peers * 32, 128)
    both = jnp.dot(
        jnp.concatenate([high, low], axis=0).astype(jnp.bfloat16),
        table,
        preferred_element_type=jnp.float32,
    )
    attended = (both[:8] + both[8:]).astype(jnp.bfloat16)
    for k in range(out_ref.shape[0]):
        out_ref[k] = attended


def project_kernel(attended_ref, weight_ref, out_ref):
    rows = attended_ref.shape[0] * attended_ref.shape[1]
    seqs = rows // 4
    flat = attended_ref[...].reshape(rows, 128)
    row, col = iota((rows, rows), 0), iota((rows, rows), 1)
    pick = jnp.where(col == (row % seqs) * 4 + row // seqs, 1.0, 0.0).astype(jnp.bfloat16)
    ordered = jnp.dot(pick, flat, preferred_element_type=jnp.float32)
    lines = jnp.concatenate([ordered[seqs * h : seqs * h + seqs] for h in range(4)], axis=1)
    mixed = jnp.dot(
        lines.astype(jnp.bfloat16), weight_ref[...], preferred_element_type=jnp.float32
    )
    for j in range(out_ref.shape[1]):
        out_ref[:, j, :] = mixed[:, 128 * j : 128 * j + 128]


def sum_kernel(parts_ref, out_ref):
    total = jnp.sum(parts_ref[...], axis=0).astype(jnp.bfloat16)
    for j in range(total.shape[0]):
        out_ref[0:1, 128 * j : 128 * j + 128] = total[j : j + 1]


def call(kernel, shape, dtype, count, scratch=(), specs=None, limit=8, flops=0, name=None):
    return pl.pallas_call(
        kernel,
        out_shape=jax.ShapeDtypeStruct(shape, dtype),
        in_specs=specs or whole(count),
        out_specs=pl.BlockSpec(memory_space=VMEM),
        scratch_shapes=list(scratch),
        compiler_params=pltpu.CompilerParams(vmem_limit_bytes=limit * MIB),
        name=name,
    )


def exchange(value, axis):
    return lax.all_to_all(value, axis, 0, 0, tiled=True)


def body(
    query, cache_keys, cache_values, new_keys, new_values, key_up, value_up, out_weight, lengths
):
    peers, groups = lax.axis_size("seq"), lax.axis_size("batch")
    length, rank = cache_keys.shape[1], cache_keys.shape[2]
    ranks, columns = key_up.shape[0], out_weight.shape[1]
    scale = query.shape[2] ** -0.5
    shift = (lax.axis_index("seq") * length).astype(jnp.int32).reshape(1)
    latent = call(latent_kernel, (peers, ranks, 256), jnp.bfloat16, 2, name="latent")(
        query, key_up
    )
    latent = exchange(latent, "seq")
    smem = [pl.BlockSpec(memory_space=pltpu.SMEM)] * 2
    parts = call(
        functools.partial(attend_kernel, scale),
        (peers, 72, 128),
        jnp.bfloat16,
        8,
        scratch=[VMEM((length, 128), jnp.float32), VMEM((128, length), jnp.bfloat16)],
        specs=smem + whole(6),
        limit=24,
        name="attend",
    )(shift, lengths, latent, cache_keys, cache_values, new_keys, new_values, value_up)
    parts = exchange(parts, "seq")
    attended = call(merge_kernel, (groups, 8, 128), jnp.bfloat16, 1, name="merge")(parts)
    attended = exchange(attended, "batch")
    mixed = call(project_kernel, (peers, columns // 128, 128), jnp.float32, 2, name="project")(
        attended, out_weight
    )
    mixed = exchange(mixed, "seq")
    return call(sum_kernel, (1, columns), jnp.bfloat16, 1, name="total")(mixed)


def solution(mesh):
    return jax.shard_map(
        body,
        mesh=mesh,
        in_specs=(
            P("batch", None, None),
            P("batch", "seq", None),
            P("batch", "seq", None),
            P("batch", None),
            P("batch", None),
            P("seq", None),
            P("seq", None),
            P("seq", "batch"),
            P("batch"),
        ),
        out_specs=P("seq", "batch"),
        check_vma=False,
    )
```

time: 104 us -> 63.1 us (0.61)
  blocking collectives: 48.2 us -> 31.7 us
  matrix products: 14.7 us -> 0 us
  other arithmetic: 6.65 us -> 0 us
  Pallas kernels: 0 us -> 5.09 us
  local copies, waits for them, and re-layouts: 13.8 us -> 8.83 us
  starting transfers between devices: 11.8 us -> 8.16 us
    all_gather x2 -> x0, blocking collectives: 25.7 us -> none  [all_in_one(): both, at, found = (lax.all_gather(jnp.concatenate(lines), axis), 0, {})]
    dot_general x7 -> x0, matrix products: 14.7 us -> none  [the longest x1 6.18 us: body(): jnp.einsum('bkgr,blr->bkgl', query_latent, cache_keys, precision=TOP_PREC...]
    all_to_all x2 -> x3, blocking collectives: 22.5 us -> 31.7 us  [exchange(): return lax.all_to_all(value, axis, 0, 0, tiled=True)]
    pallas_call x0 -> x5, Pallas kernels: none -> 5.09 us  [the longest x1 2.75 us: body(): call(functools.partial(attend_kernel, scale), (peers, 72, 128), jnp.bfloa...]
    all_to_all x2 -> x1, starting transfers between devices: 11.8 us -> 8.16 us  [exchange(): return lax.all_to_all(value, axis, 0, 0, tiled=True)]
    unnamed x19 -> x18, local copies, waits for them, and re-layouts: 5.21 us -> 8.83 us
    reshape x5 -> x0, local copies, waits for them, and re-layouts: 2.34 us -> none  [the longest x2 1.65 us: in_order(): return jnp.moveaxis(pieces, 0, dim).reshape(shape)]
    broadcast_in_dim x3 -> x0, local copies, waits for them, and re-layouts: 2.09 us -> none  [from_everyone(): jnp.broadcast_to(value[None], (size, *value.shape))]
  transfers between devices with their start and end apart: 2 -> 1, of which waited for: 1 -> 1; matrix products, arithmetic and copies ran while one was open for 19% -> 0% of each run, Pallas kernels for 0% -> 0%
where the time goes in v1:
time: 63.1 us; the launch traced here: 62.6 us
  blocking collectives  31.7 us (50%)
  local copies, waits for them, and re-layouts  8.83 us (14%)
  waiting for transfers between devices  8.69 us (14%)
  starting transfers between devices  8.16 us (13%)
  Pallas kernels  5.09 us (8%)
    all_to_all x3, blocking collectives, exchange(): return lax.all_to_all(value, axis, 0, 0, tiled=True)  31.7 us
    unnamed x18, local copies, waits for them, and re-layouts  8.83 us
    all_to_all x1, waiting for transfers between devices, exchange(): return lax.all_to_all(value, axis, 0, 0, tiled=True)  8.69 us
    all_to_all x1, starting transfers between devices, exchange(): return lax.all_to_all(value, axis, 0, 0, tiled=True)  8.16 us
    pallas_call x1, Pallas kernels, body(): call(functools.partial(attend_kernel, scale), (peers, 72, 128), jnp.bfloa...  2.75 us
  transfers between devices with their start and end apart: 1, of which 1 were waited for; matrix products, arithmetic and copies ran while one was open for 0% of the time, Pallas kernels for 0%

profile of v1, /device:TPU:0, one launch (start us, length us, event | category | flops | bytes accessed | tf_op | source)
XLA Modules:
  0.0 62.6 jit_solution(376988425615907664)
XLA Ops:
  0.0 0.0 copy-start.4
  0.0 0.8 %copy-done.4 = bf16[32,1024]{1,0:T(8,128)(2,1)S(1)} copy-done((bf16[32,1024]{1,0:T(8,128)(2,1)S(1)}, bf16[32,1024]{1,0:T(8,128)(2,1)}, u32[]{:S(2)}) %copy-start.4) | copy-done | bytes 65560
  0.8 0.0 copy-start.5
  0.8 0.8 %copy-done.5 = bf16[2,64,128]{2,1,0:T(8,128)(2,1)S(1)} copy-done((bf16[2,64,128]{2,1,0:T(8,128)(2,1)S(1)}, bf16[2,64,128]{2,1,0:T(8,128)(2,1)}, u32[]{:S(2)}) %copy-start.5) | copy-done | bytes 32792
  1.6 1.1 %latent.1 = bf16[16,32,256]{2,1,0:T(8,128)(2,1)} custom-call(bf16[2,64,128]{2,1,0:T(8,128)(2,1)S(1)} %copy-done.5, bf16[32,1024]{1,0:T(8,128)(2,1)S(1)} %copy-done.4), custom_call_target="tpu_custom_call" | custom-call | tf_op jit(solution)/shard_map/latent/pallas_call | solution.py:203
  2.7 8.2 %all-to-all-start = ((bf16[16,32,256]{2,1,0:T(8,128)(2,1)}), bf16[16,32,256]{2,1,0:T(8,128)(2,1)S(1)}, u32[]{:S(2)}, u32[]{:S(2)}) async-start(bf16[16,32,256]{2,1,0:T(8,128)(2,1)} %latent.1), calls=%async_computation | async-start | bytes 524288 | tf_op jit(solution)/shard_map/all_to_all | solution.py:192
  10.8 8.7 %all-to-all-done.latent_ref = bf16[16,32,256]{2,1,0:T(8,128)(2,1)S(1)} async-done(((bf16[16,32,256]{2,1,0:T(8,128)(2,1)}), bf16[16,32,256]{2,1,0:T(8,128)(2,1)S(1)}, u32[]{:S(2)}, u32[]{:S(2)}) %all-to-all-start) | async-done | bytes 262176 | tf_op jit(solution)/shard_map/all_to_all | solution.py:192
  19.5 0.0 copy-start
  19.5 2.2 %copy-done = bf16[2,2048,512]{2,1,0:T(8,128)(2,1)S(1)} copy-done((bf16[2,2048,512]{2,1,0:T(8,128)(2,1)S(1)}, bf16[2,2048,512]{2,1,0:T(8,128)(2,1)}, u32[]{:S(2)}) %copy-start) | copy-done | bytes 4194328
  21.7 0.0 copy-start.1
  21.7 2.2 %copy-done.1 = bf16[2,2048,512]{2,1,0:T(8,128)(2,1)S(1)} copy-done((bf16[2,2048,512]{2,1,0:T(8,128)(2,1)S(1)}, bf16[2,2048,512]{2,1,0:T(8,128)(2,1)}, u32[]{:S(2)}) %copy-start.1) | copy-done | bytes 4194328
  23.9 0.8 %copy-done.3 = bf16[32,1024]{1,0:T(8,128)(2,1)S(1)} copy-done((bf16[32,1024]{1,0:T(8,128)(2,1)S(1)}, bf16[32,1024]{1,0:T(8,128)(2,1)}, u32[]{:S(2)}) %copy-start.3) | copy-done | bytes 65560
  24.7 0.7 %copy-done.6 = bf16[2,512]{1,0:T(2,128)(2,1)S(1)} copy-done((bf16[2,512]{1,0:T(2,128)(2,1)S(1)}, bf16[2,512]{1,0:T(2,128)(2,1)}, u32[]{:S(2)}) %copy-start.6) | copy-done | bytes 2072
  25.4 0.0 copy-start.7
  25.4 0.7 %copy-done.7 = bf16[2,512]{1,0:T(2,128)(2,1)S(1)} copy-done((bf16[2,512]{1,0:T(2,128)(2,1)S(1)}, bf16[2,512]{1,0:T(2,128)(2,1)}, u32[]{:S(2)}) %copy-start.7) | copy-done | bytes 2072
  26.1 0.7 %copy-done.8 = s32[2]{0:T(128)S(1)} copy-done((s32[2]{0:T(128)S(1)}, s32[2]{0:T(128)}, u32[]{:S(2)}) %copy-start.8) | copy-done | bytes 32
  26.8 2.8 %attend.1 = bf16[16,72,128]{2,1,0:T(8,128)(2,1)S(1)} custom-call(s32[1]{0:T(128)} %bitcast.shift_ref, s32[2]{0:T(128)S(1)} %copy-done.8, bf16[16,32,256]{2,1,0:T(8,128)(2,1)S(1)} %all-to-all-done.latent_ref, bf16[2,2048,512]{2,1,0:T(8,128)(2,1)S(1)} %copy-done, bf16[2,2048,512]{2,1,0:T(8,128)(2,1)S(1)} %copy-done.1, bf16[2,512]{1,0:T(2,128)(2,1)S(1)} %copy-done.6, ...), custom_call_target="tpu_custom_call" | custom-call | tf_op jit(solution)/shard_map/attend/pallas_call | solution.py:208
  29.5 11.8 %all_to_all.20.parts_ref = bf16[16,72,128]{2,1,0:T(8,128)(2,1)S(1)} all-to-all(bf16[16,72,128]{2,1,0:T(8,128)(2,1)S(1)} %attend.1), channel_id=1, replica_groups=mesh['batch'=8,'seq'=16] {'seq'}, dimensions={0} | all-to-all | bytes 589824 | tf_op jit(solution)/shard_map/all_to_all | solution.py:192
  41.3 0.3 merge.1
  41.6 9.4 %all_to_all.21.attended_ref = bf16[8,8,128]{2,1,0:T(8,128)(2,1)S(1)} all-to-all(bf16[8,8,128]{2,1,0:T(8,128)(2,1)S(1)} %merge.1), channel_id=1, replica_groups=mesh['batch'=8,'seq'=16] {'batch'}, dimensions={0} | all-to-all | bytes 32768 | tf_op jit(solution)/shard_map/all_to_all | solution.py:192
  51.1 0.0 copy-done.2
  51.1 0.4 project.1
  51.4 10.5 %all_to_all.22.parts_ref = f32[16,8,128]{2,1,0:T(8,128)S(1)} all-to-all(f32[16,8,128]{2,1,0:T(8,128)S(1)} %project.1), channel_id=1, replica_groups=mesh['batch'=8,'seq'=16] {'seq'}, dimensions={0} | all-to-all | bytes 131072 | tf_op jit(solution)/shard_map/all_to_all | solution.py:192
  61.9 0.6 total.1
  (4 shorter events, 0.0 us)
Async XLA Ops:
  0.0 0.8 %copy-start.4 = (bf16[32,1024]{1,0:T(8,128)(2,1)S(1)}, bf16[32,1024]{1,0:T(8,128)(2,1)}, u32[]{:S(2)}) copy-start(bf16[32,1024]{1,0:T(8,128)(2,1)} %key_up_ref.1) | copy-start | bytes 196612
  0.8 0.8 %copy-start.5 = (bf16[2,64,128]{2,1,0:T(8,128)(2,1)S(1)}, bf16[2,64,128]{2,1,0:T(8,128)(2,1)}, u32[]{:S(2)}) copy-start(bf16[2,64,128]{2,1,0:T(8,128)(2,1)} %query_ref.1) | copy-start | bytes 98308
  2.7 16.9 %all-to-all-start = ((bf16[16,32,256]{2,1,0:T(8,128)(2,1)}), bf16[16,32,256]{2,1,0:T(8,128)(2,1)S(1)}, u32[]{:S(2)}, u32[]{:S(2)}) async-start(bf16[16,32,256]{2,1,0:T(8,128)(2,1)} %latent.1), calls=%async_computation | async-start | bytes 524288 | tf_op jit(solution)/shard_map/all_to_all | solution.py:192
  19.5 2.2 %copy-start = (bf16[2,2048,512]{2,1,0:T(8,128)(2,1)S(1)}, bf16[2,2048,512]{2,1,0:T(8,128)(2,1)}, u32[]{:S(2)}) copy-start(bf16[2,2048,512]{2,1,0:T(8,128)(2,1)} %keys_ref.1) | copy-start | bytes 12582916
  21.7 2.2 %copy-start.1 = (bf16[2,2048,512]{2,1,0:T(8,128)(2,1)S(1)}, bf16[2,2048,512]{2,1,0:T(8,128)(2,1)}, u32[]{:S(2)}) copy-start(bf16[2,2048,512]{2,1,0:T(8,128)(2,1)} %values_ref.1) | copy-start | bytes 12582916
  23.9 0.8 %copy-start.3 = (bf16[32,1024]{1,0:T(8,128)(2,1)S(1)}, bf16[32,1024]{1,0:T(8,128)(2,1)}, u32[]{:S(2)}) copy-start(bf16[32,1024]{1,0:T(8,128)(2,1)} %value_up_ref.1) | copy-start | bytes 196612
  24.7 0.7 %copy-start.6 = (bf16[2,512]{1,0:T(2,128)(2,1)S(1)}, bf16[2,512]{1,0:T(2,128)(2,1)}, u32[]{:S(2)}) copy-start(bf16[2,512]{1,0:T(2,128)(2,1)} %new_keys_ref.1) | copy-start | bytes 6148
  25.4 0.7 %copy-start.7 = (bf16[2,512]{1,0:T(2,128)(2,1)S(1)}, bf16[2,512]{1,0:T(2,128)(2,1)}, u32[]{:S(2)}) copy-start(bf16[2,512]{1,0:T(2,128)(2,1)} %new_values_ref.1) | copy-start | bytes 6148
  26.1 0.7 %copy-start.8 = (s32[2]{0:T(128)S(1)}, s32[2]{0:T(128)}, u32[]{:S(2)}) copy-start(s32[2]{0:T(128)} %lengths_ref.1) | copy-start | bytes 28
  26.8 24.3 %copy-start.2 = (bf16[512,1024]{1,0:T(8,128)(2,1)S(1)}, bf16[512,1024]{1,0:T(8,128)(2,1)}, u32[]{:S(2)}) copy-start(bf16[512,1024]{1,0:T(8,128)(2,1)} %weight_ref.1) | copy-start | bytes 3145732

commit v2 on v1

--- a/solution.py
+++ b/solution.py
@@ -11,6 +11,7 @@
 FLOOR = -1e20
 VMEM = pltpu.VMEM
 MIB = 1024 * 1024
+LEAD, LATENT = 2 * 10**10, 2 * 10**10
 
 
 def iota(shape, dim):
@@ -26,8 +27,11 @@
     return high, value - high
 
 
-def latent_kernel(query_ref, key_up_ref, out_ref):
-    peers, ranks, _ = out_ref.shape
+def lead_kernel(out_ref):
+    out_ref[...] = jnp.zeros_like(out_ref)
+
+
+def latent_kernel(lead_ref, query_ref, key_up_ref, out_ref):
     flat = query_ref[...].reshape(128, 128)
     row, col = iota((128, 128), 0), iota((128, 128), 1)
     source = ((row >> 2) & 1) * 64 + (row >> 3) * 4 + (row & 3)
@@ -44,13 +48,12 @@
     )
     high, low = split(latent)
     piece = jnp.concatenate([high, low], axis=1).astype(jnp.bfloat16)
-    for k in range(peers):
+    for k in range(out_ref.shape[0]):
         out_ref[k] = piece
 
 
 def attend_kernel(
     scale,
-    shift_ref,
     lengths_ref,
     latent_ref,
     keys_ref,
@@ -66,7 +69,7 @@
     rank = peers * ranks
     length = keys_ref.shape[1]
     chunk = 512
-    shift = shift_ref[0]
+    shift = lax.axis_index("seq") * length
     both = latent_ref[...].reshape(rank, width)
     lane = iota((rank, width), 1)
     maps = [
@@ -176,14 +179,17 @@
         out_ref[0:1, 128 * j : 128 * j + 128] = total[j : j + 1]
 
 
-def call(kernel, shape, dtype, count, scratch=(), specs=None, limit=8, flops=0, name=None):
+def call(kernel, outs, count, scratch=(), specs=None, limit=8, flops=0, name=None):
+    outs = [jax.ShapeDtypeStruct(*out) for out in outs]
+    one = len(outs) == 1
     return pl.pallas_call(
         kernel,
-        out_shape=jax.ShapeDtypeStruct(shape, dtype),
-        in_specs=specs or whole(count),
-        out_specs=pl.BlockSpec(memory_space=VMEM),
+        out_shape=outs[0] if one else outs,
+        in_specs=whole(count) if specs is None else specs,
+        out_specs=whole(1)[0] if one else whole(len(outs)),
         scratch_shapes=list(scratch),
         compiler_params=pltpu.CompilerParams(vmem_limit_bytes=limit * MIB),
+        cost_estimate=pl.CostEstimate(flops=flops, bytes_accessed=0, transcendentals=0),
         name=name,
     )
 
@@ -199,30 +205,31 @@
     length, rank = cache_keys.shape[1], cache_keys.shape[2]
     ranks, columns = key_up.shape[0], out_weight.shape[1]
     scale = query.shape[2] ** -0.5
-    shift = (lax.axis_index("seq") * length).astype(jnp.int32).reshape(1)
-    latent = call(latent_kernel, (peers, ranks, 256), jnp.bfloat16, 2, name="latent")(
-        query, key_up
-    )
+    f32, bf16 = jnp.float32, jnp.bfloat16
+    lead = call(lead_kernel, [((8, 128), f32)], 0, limit=4, flops=LEAD, name="lead")()
+    latent = call(
+        latent_kernel, [((peers, ranks, 256), bf16)], 3, limit=4, flops=LATENT, name="latent"
+    )(lead, query, key_up)
     latent = exchange(latent, "seq")
-    smem = [pl.BlockSpec(memory_space=pltpu.SMEM)] * 2
+    smem = [pl.BlockSpec(memory_space=pltpu.SMEM)]
     parts = call(
         functools.partial(attend_kernel, scale),
-        (peers, 72, 128),
-        jnp.bfloat16,
-        8,
-        scratch=[VMEM((length, 128), jnp.float32), VMEM((128, length), jnp.bfloat16)],
+        [((peers, 72, 128), bf16)],
+        7,
+        scratch=[VMEM((length, 128), f32), VMEM((128, length), bf16)],
         specs=smem + whole(6),
-        limit=24,
+        limit=16,
+        flops=10**9,
         name="attend",
-    )(shift, lengths, latent, cache_keys, cache_values, new_keys, new_values, value_up)
+    )(lengths, latent, cache_keys, cache_values, new_keys, new_values, value_up)
     parts = exchange(parts, "seq")
-    attended = call(merge_kernel, (groups, 8, 128), jnp.bfloat16, 1, name="merge")(parts)
+    attended = call(merge_kernel, [((groups, 8, 128), bf16)], 1, name="merge")(parts)
     attended = exchange(attended, "batch")
-    mixed = call(project_kernel, (peers, columns // 128, 128), jnp.float32, 2, name="project")(
+    mixed = call(project_kernel, [((peers, columns // 128, 128), f32)], 2, name="project")(
         attended, out_weight
     )
     mixed = exchange(mixed, "seq")
-    return call(sum_kernel, (1, columns), jnp.bfloat16, 1, name="total")(mixed)
+    return call(sum_kernel, [((1, columns), bf16)], 1, name="total")(mixed)
 
 
 def solution(mesh):

time: 63.1 us -> 54.3 us (0.86)
  blocking collectives: 31.7 us -> 48.7 us
  waiting for transfers between devices: 8.69 us -> 0 us
  starting transfers between devices: 8.16 us -> 0 us
  local copies, waits for them, and re-layouts: 8.83 us -> 0.87 us
  Pallas kernels: 5.09 us -> 4.44 us
    all_to_all x3 -> x4, blocking collectives: 31.7 us -> 48.7 us  [exchange(): return lax.all_to_all(value, axis, 0, 0, tiled=True)]
    all_to_all x1 -> x0, waiting for transfers between devices: 8.69 us -> none  [exchange(): return lax.all_to_all(value, axis, 0, 0, tiled=True)]
    all_to_all x1 -> x0, starting transfers between devices: 8.16 us -> none  [exchange(): return lax.all_to_all(value, axis, 0, 0, tiled=True)]
    unnamed x18, local copies, waits for them, and re-layouts: 8.83 us -> 0.87 us
    pallas_call x5 -> x6, Pallas kernels: 5.09 us -> 4.44 us  [the longest x1 2.81 us: body(): call(functools.partial(attend_kernel, scale), [((peers, 72, 128), bf16)],...]
  transfers between devices with their start and end apart: 1 -> 0, of which waited for: 1 -> 0; matrix products, arithmetic and copies ran while one was open for 0% -> 0% of each run, Pallas kernels for 0% -> 0%
where the time goes in v2:
time: 54.3 us; the launch traced here: 54.1 us
  blocking collectives  48.7 us (90%)
  Pallas kernels  4.44 us (8%)
  local copies, waits for them, and re-layouts  0.87 us (2%)
    all_to_all x4, blocking collectives, exchange(): return lax.all_to_all(value, axis, 0, 0, tiled=True)  48.7 us
    pallas_call x1, Pallas kernels, body(): call(functools.partial(attend_kernel, scale), [((peers, 72, 128), bf16)],...  2.81 us

profile of v2, /device:TPU:0, one launch (start us, length us, event | category | flops | bytes accessed | tf_op | source)
XLA Modules:
  0.0 54.1 jit_solution(17143749448785158256)
XLA Ops:
  0.0 0.0 copy-start.7
  0.0 0.8 %copy-done.7 = bf16[32,1024]{1,0:T(8,128)(2,1)S(1)} copy-done((bf16[32,1024]{1,0:T(8,128)(2,1)S(1)}, bf16[32,1024]{1,0:T(8,128)(2,1)}, u32[]{:S(2)}) %copy-start.7) | copy-done | bytes 65560
  0.8 0.0 copy-done.8
  0.8 0.0 copy-start
  0.9 0.0 copy-start.4
  0.9 0.0 copy-start.5
  0.9 0.0 copy-start.6
  0.9 0.3 latent.1
  1.2 16.9 %all_to_all.20.latent_ref = bf16[16,32,256]{2,1,0:T(8,128)(2,1)S(1)} all-to-all(bf16[16,32,256]{2,1,0:T(8,128)(2,1)S(1)} %latent.1), channel_id=1, replica_groups=mesh['batch'=8,'seq'=16] {'seq'}, dimensions={0} | all-to-all | bytes 524288 | tf_op jit(solution)/shard_map/all_to_all | solution.py:198
  18.2 0.0 copy-done
  18.2 0.0 copy-done.1
  18.2 0.0 copy-done.3
  18.2 0.0 copy-done.4
  18.2 0.0 copy-done.5
  18.2 0.0 copy-done.6
  18.2 0.0 copy-start.2
  18.2 2.8 %attend.1 = bf16[16,72,128]{2,1,0:T(8,128)(2,1)S(1)} custom-call(s32[2]{0:T(128)S(1)} %copy-done.6, bf16[16,32,256]{2,1,0:T(8,128)(2,1)S(1)} %all_to_all.20.latent_ref, bf16[2,2048,512]{2,1,0:T(8,128)(2,1)S(1)} %copy-done, bf16[2,2048,512]{2,1,0:T(8,128)(2,1)S(1)} %copy-done.1, bf16[2,512]{1,0:T(2,128)(2,1)S(1)} %copy-done.4, bf16[2,512]{1,0:T(2,128)(2,1)S(1)} %copy-done.5, ...), custom_call_target="tpu_custom_call" | custom-call | flops 1000000000 | tf_op jit(solution)/shard_map/attend/pallas_call | solution.py:215
  21.0 11.8 %all_to_all.21.parts_ref = bf16[16,72,128]{2,1,0:T(8,128)(2,1)S(1)} all-to-all(bf16[16,72,128]{2,1,0:T(8,128)(2,1)S(1)} %attend.1), channel_id=1, replica_groups=mesh['batch'=8,'seq'=16] {'seq'}, dimensions={0} | all-to-all | bytes 589824 | tf_op jit(solution)/shard_map/all_to_all | solution.py:198
  32.8 0.3 merge.1
  33.1 9.5 %all_to_all.22.attended_ref = bf16[8,8,128]{2,1,0:T(8,128)(2,1)S(1)} all-to-all(bf16[8,8,128]{2,1,0:T(8,128)(2,1)S(1)} %merge.1), channel_id=1, replica_groups=mesh['batch'=8,'seq'=16] {'batch'}, dimensions={0} | all-to-all | bytes 32768 | tf_op jit(solution)/shard_map/all_to_all | solution.py:198
  42.6 0.0 copy-done.2
  42.6 0.4 project.1
  42.9 10.5 %all_to_all.23.parts_ref = f32[16,8,128]{2,1,0:T(8,128)S(1)} all-to-all(f32[16,8,128]{2,1,0:T(8,128)S(1)} %project.1), channel_id=1, replica_groups=mesh['batch'=8,'seq'=16] {'seq'}, dimensions={0} | all-to-all | bytes 131072 | tf_op jit(solution)/shard_map/all_to_all | solution.py:198
  53.5 0.6 %total.1 = bf16[1,1024]{1,0:T(2,128)(2,1)} custom-call(f32[16,8,128]{2,1,0:T(8,128)S(1)} %all_to_all.23.parts_ref), custom_call_target="tpu_custom_call" | custom-call | tf_op jit(solution)/shard_map/total/pallas_call | solution.py:232
  (4 shorter events, 0.0 us)
Async XLA Ops:
  0.0 0.8 %copy-start.7 = (bf16[32,1024]{1,0:T(8,128)(2,1)S(1)}, bf16[32,1024]{1,0:T(8,128)(2,1)}, u32[]{:S(2)}) copy-start(bf16[32,1024]{1,0:T(8,128)(2,1)} %key_up_ref.1) | copy-start | bytes 196612
  0.0 0.8 %copy-start.8 = (bf16[2,64,128]{2,1,0:T(8,128)(2,1)S(1)}, bf16[2,64,128]{2,1,0:T(8,128)(2,1)}, u32[]{:S(2)}) copy-start(bf16[2,64,128]{2,1,0:T(8,128)(2,1)} %query_ref.1) | copy-start | bytes 98308
  0.8 17.3 %copy-start = (bf16[2,2048,512]{2,1,0:T(8,128)(2,1)S(1)}, bf16[2,2048,512]{2,1,0:T(8,128)(2,1)}, u32[]{:S(2)}) copy-start(bf16[2,2048,512]{2,1,0:T(8,128)(2,1)} %keys_ref.1) | copy-start | bytes 12582916
  0.8 17.3 %copy-start.1 = (bf16[2,2048,512]{2,1,0:T(8,128)(2,1)S(1)}, bf16[2,2048,512]{2,1,0:T(8,128)(2,1)}, u32[]{:S(2)}) copy-start(bf16[2,2048,512]{2,1,0:T(8,128)(2,1)} %values_ref.1) | copy-start | bytes 12582916
  0.8 17.3 %copy-start.3 = (bf16[32,1024]{1,0:T(8,128)(2,1)S(1)}, bf16[32,1024]{1,0:T(8,128)(2,1)}, u32[]{:S(2)}) copy-start(bf16[32,1024]{1,0:T(8,128)(2,1)} %value_up_ref.1) | copy-start | bytes 196612
  0.9 17.3 %copy-start.4 = (bf16[2,512]{1,0:T(2,128)(2,1)S(1)}, bf16[2,512]{1,0:T(2,128)(2,1)}, u32[]{:S(2)}) copy-start(bf16[2,512]{1,0:T(2,128)(2,1)} %new_keys_ref.1) | copy-start | bytes 6148
  0.9 17.3 %copy-start.5 = (bf16[2,512]{1,0:T(2,128)(2,1)S(1)}, bf16[2,512]{1,0:T(2,128)(2,1)}, u32[]{:S(2)}) copy-start(bf16[2,512]{1,0:T(2,128)(2,1)} %new_values_ref.1) | copy-start | bytes 6148
  0.9 17.3 %copy-start.6 = (s32[2]{0:T(128)S(1)}, s32[2]{0:T(128)}, u32[]{:S(2)}) copy-start(s32[2]{0:T(128)} %lengths_ref.1) | copy-start | bytes 28
  18.2 24.4 %copy-start.2 = (bf16[512,1024]{1,0:T(8,128)(2,1)S(1)}, bf16[512,1024]{1,0:T(8,128)(2,1)}, u32[]{:S(2)}) copy-start(bf16[512,1024]{1,0:T(8,128)(2,1)} %weight_ref.1) | copy-start | bytes 3145732

commit v3 on v2

--- a/solution.py
+++ b/solution.py
@@ -12,6 +12,7 @@
 VMEM = pltpu.VMEM
 MIB = 1024 * 1024
 LEAD, LATENT = 2 * 10**10, 2 * 10**10
+FIRST = (10, 10, 5, 10)
 
 
 def iota(shape, dim):
@@ -70,7 +71,7 @@
     length = keys_ref.shape[1]
     chunk = 512
     shift = lax.axis_index("seq") * length
-    both = latent_ref[...].reshape(rank, width)
+    both = jnp.concatenate([latent_ref[swapped(k, FIRST[0])] for k in range(peers)], axis=0)
     lane = iota((rank, width), 1)
     maps = [
         jnp.where(((lane >> 2) & 1) == b, both.astype(jnp.float32), 0.0).astype(jnp.bfloat16)
@@ -122,9 +123,10 @@
     for k in range(peers):
         lines = summed[8 * k : 8 * k + 8]
         stack = [lines[:, 128 * g : 128 * g + 128] for g in range(rank // 128)]
-        out_ref[k, 0:32, :] = jnp.concatenate(stack, axis=0).astype(jnp.bfloat16)
-        out_ref[k, 32:64, :] = value_up_ref[:, 128 * (k // 2) : 128 * (k // 2) + 128]
-        out_ref[k, 64:72, :] = table[8 * k : 8 * k + 8].astype(jnp.bfloat16)
+        to = swapped(k, FIRST[1])
+        out_ref[to, 0:32, :] = jnp.concatenate(stack, axis=0).astype(jnp.bfloat16)
+        out_ref[to, 32:64, :] = value_up_ref[:, 128 * (k // 2) : 128 * (k // 2) + 128]
+        out_ref[to, 64:72, :] = table[8 * k : 8 * k + 8].astype(jnp.bfloat16)
 
 
 def merge_kernel(parts_ref, out_ref):
@@ -147,10 +149,10 @@
             sums[g] += factor * lines[8 * g : 8 * g + 8]
     latent = jnp.concatenate([s / total for s in sums], axis=1)
     high, low = split(latent)
-    table = parts_ref[:, 32:64, :].reshape(peers * 32, 128)
+    table = [parts_ref[swapped(k, FIRST[1]), 32:64, :] for k in range(peers)]
     both = jnp.dot(
         jnp.concatenate([high, low], axis=0).astype(jnp.bfloat16),
-        table,
+        jnp.concatenate(table, axis=0),
         preferred_element_type=jnp.float32,
     )
     attended = (both[:8] + both[8:]).astype(jnp.bfloat16)
@@ -163,7 +165,12 @@
     seqs = rows // 4
     flat = attended_ref[...].reshape(rows, 128)
     row, col = iota((rows, rows), 0), iota((rows, rows), 1)
-    pick = jnp.where(col == (row % seqs) * 4 + row // seqs, 1.0, 0.0).astype(jnp.bfloat16)
+    seq, head = row % seqs, row // seqs
+    seq = jnp.where(seq == 0, FIRST[3], jnp.where(seq == FIRST[3], 0, seq))
+    group, within = seq >> 1, seq & 1
+    group = jnp.where(group == 0, FIRST[2], jnp.where(group == FIRST[2], 0, group))
+    source = (group * 2 + within) * 4 + head
+    pick = jnp.where(col == source, 1.0, 0.0).astype(jnp.bfloat16)
     ordered = jnp.dot(pick, flat, preferred_element_type=jnp.float32)
     lines = jnp.concatenate([ordered[seqs * h : seqs * h + seqs] for h in range(4)], axis=1)
     mixed = jnp.dot(
@@ -194,8 +201,13 @@
     )
 
 
-def exchange(value, axis):
-    return lax.all_to_all(value, axis, 0, 0, tiled=True)
+def swapped(k, first):
+    return first if k == 0 else 0 if k == first else k
+
+
+def exchange(value, axis, first):
+    order = [swapped(k, first) for k in range(lax.axis_size(axis))]
+    return lax.all_to_all(value, axis, 0, 0, axis_index_groups=[order], tiled=True)
 
 
 def body(
@@ -210,7 +222,7 @@
     latent = call(
         latent_kernel, [((peers, ranks, 256), bf16)], 3, limit=4, flops=LATENT, name="latent"
     )(lead, query, key_up)
-    latent = exchange(latent, "seq")
+    latent = exchange(latent, "seq", FIRST[0])
     smem = [pl.BlockSpec(memory_space=pltpu.SMEM)]
     parts = call(
         functools.partial(attend_kernel, scale),
@@ -222,13 +234,13 @@
         flops=10**9,
         name="attend",
     )(lengths, latent, cache_keys, cache_values, new_keys, new_values, value_up)
-    parts = exchange(parts, "seq")
+    parts = exchange(parts, "seq", FIRST[1])
     attended = call(merge_kernel, [((groups, 8, 128), bf16)], 1, name="merge")(parts)
-    attended = exchange(attended, "batch")
+    attended = exchange(attended, "batch", FIRST[2])
     mixed = call(project_kernel, [((peers, columns // 128, 128), f32)], 2, name="project")(
         attended, out_weight
     )
-    mixed = exchange(mixed, "seq")
+    mixed = exchange(mixed, "seq", FIRST[3])
     return call(sum_kernel, [((1, columns), bf16)], 1, name="total")(mixed)
 
 

time: 54.3 us -> 48.5 us (0.89)
  blocking collectives: 48.7 us -> 42.8 us
    all_to_all x4, blocking collectives: 48.7 us -> 42.8 us  [exchange(): lax.all_to_all(value, axis, 0, 0, axis_index_groups=[order], tiled=True)]
where the time goes in v3:
time: 48.5 us; the launch traced here: 48.2 us
  blocking collectives  42.8 us (88%)
  Pallas kernels  4.45 us (9%)
  local copies, waits for them, and re-layouts  0.87 us (2%)
    all_to_all x4, blocking collectives, exchange(): lax.all_to_all(value, axis, 0, 0, axis_index_groups=[order], tiled=True)  42.8 us
    pallas_call x1, Pallas kernels, body(): call(functools.partial(attend_kernel, scale), [((peers, 72, 128), bf16)],...  2.81 us

profile of v3, /device:TPU:0, one launch (start us, length us, event | category | flops | bytes accessed | tf_op | source)
XLA Modules:
  0.0 48.2 jit_solution(18006719098259926587)
XLA Ops:
  0.0 0.0 copy-start.7
  0.0 0.0 copy-start.8
  0.0 0.8 %copy-done.7 = bf16[32,1024]{1,0:T(8,128)(2,1)S(1)} copy-done((bf16[32,1024]{1,0:T(8,128)(2,1)S(1)}, bf16[32,1024]{1,0:T(8,128)(2,1)}, u32[]{:S(2)}) %copy-start.7) | copy-done | bytes 65560
  0.8 0.0 copy-done.8
  0.9 0.0 copy-start.4
  0.9 0.0 copy-start.5
  0.9 0.0 copy-start.6
  0.9 0.3 latent.1
  1.2 14.1 %all_to_all.20.latent_ref = bf16[16,32,256]{2,1,0:T(8,128)(2,1)S(1)} all-to-all(bf16[16,32,256]{2,1,0:T(8,128)(2,1)S(1)} %latent.1), channel_id=1, replica_groups={{10,1,2,3,4,5,6,7,8,9,0,11,12,13,14,15},{26,17,18,19,20,21,22,23,24,25,..., dimensions={0} | all-to-all | bytes 524288 | tf_op jit(solution)/shard_map/all_to_all | solution.py:210
  15.3 0.0 copy-done
  15.3 0.0 copy-done.1
  15.3 0.0 copy-done.3
  15.4 0.0 copy-done.4
  15.4 0.0 copy-done.5
  15.4 0.0 copy-done.6
  15.4 0.0 copy-start.2
  15.4 2.8 %attend.1 = bf16[16,72,128]{2,1,0:T(8,128)(2,1)S(1)} custom-call(s32[2]{0:T(128)S(1)} %copy-done.6, bf16[16,32,256]{2,1,0:T(8,128)(2,1)S(1)} %all_to_all.20.latent_ref, bf16[2,2048,512]{2,1,0:T(8,128)(2,1)S(1)} %copy-done, bf16[2,2048,512]{2,1,0:T(8,128)(2,1)S(1)} %copy-done.1, bf16[2,512]{1,0:T(2,128)(2,1)S(1)} %copy-done.4, bf16[2,512]{1,0:T(2,128)(2,1)S(1)} %copy-done.5, ...), custom_call_target="tpu_custom_call" | custom-call | flops 1000000000 | tf_op jit(solution)/shard_map/attend/pallas_call | solution.py:227
  18.2 11.3 %all_to_all.21.parts_ref = bf16[16,72,128]{2,1,0:T(8,128)(2,1)S(1)} all-to-all(bf16[16,72,128]{2,1,0:T(8,128)(2,1)S(1)} %attend.1), channel_id=1, replica_groups={{10,1,2,3,4,5,6,7,8,9,0,11,12,13,14,15},{26,17,18,19,20,21,22,23,24,25,..., dimensions={0} | all-to-all | bytes 589824 | tf_op jit(solution)/shard_map/all_to_all | solution.py:210
  29.5 0.3 merge.1
  29.8 7.3 %all_to_all.22.attended_ref = bf16[8,8,128]{2,1,0:T(8,128)(2,1)S(1)} all-to-all(bf16[8,8,128]{2,1,0:T(8,128)(2,1)S(1)} %merge.1), channel_id=1, replica_groups={{80,16,32,48,64,0,96,112},{81,17,33,49,65,1,97,113},{82,18,34,50,66,2,9..., dimensions={0} | all-to-all | bytes 32768 | tf_op jit(solution)/shard_map/all_to_all | solution.py:210
  37.1 0.0 copy-done.2
  37.1 0.4 project.1
  37.5 10.1 %all_to_all.23.parts_ref = f32[16,8,128]{2,1,0:T(8,128)S(1)} all-to-all(f32[16,8,128]{2,1,0:T(8,128)S(1)} %project.1), channel_id=1, replica_groups={{10,1,2,3,4,5,6,7,8,9,0,11,12,13,14,15},{26,17,18,19,20,21,22,23,24,25,..., dimensions={0} | all-to-all | bytes 131072 | tf_op jit(solution)/shard_map/all_to_all | solution.py:210
  47.6 0.6 %total.1 = bf16[1,1024]{1,0:T(2,128)(2,1)} custom-call(f32[16,8,128]{2,1,0:T(8,128)S(1)} %all_to_all.23.parts_ref), custom_call_target="tpu_custom_call" | custom-call | tf_op jit(solution)/shard_map/total/pallas_call | solution.py:244
  (4 shorter events, 0.0 us)
Async XLA Ops:
  0.0 0.8 %copy-start.7 = (bf16[32,1024]{1,0:T(8,128)(2,1)S(1)}, bf16[32,1024]{1,0:T(8,128)(2,1)}, u32[]{:S(2)}) copy-start(bf16[32,1024]{1,0:T(8,128)(2,1)} %key_up_ref.1) | copy-start | bytes 196612
  0.0 0.8 %copy-start.8 = (bf16[2,64,128]{2,1,0:T(8,128)(2,1)S(1)}, bf16[2,64,128]{2,1,0:T(8,128)(2,1)}, u32[]{:S(2)}) copy-start(bf16[2,64,128]{2,1,0:T(8,128)(2,1)} %query_ref.1) | copy-start | bytes 98308
  0.8 14.5 %copy-start = (bf16[2,2048,512]{2,1,0:T(8,128)(2,1)S(1)}, bf16[2,2048,512]{2,1,0:T(8,128)(2,1)}, u32[]{:S(2)}) copy-start(bf16[2,2048,512]{2,1,0:T(8,128)(2,1)} %keys_ref.1) | copy-start | bytes 12582916
  0.8 14.5 %copy-start.1 = (bf16[2,2048,512]{2,1,0:T(8,128)(2,1)S(1)}, bf16[2,2048,512]{2,1,0:T(8,128)(2,1)}, u32[]{:S(2)}) copy-start(bf16[2,2048,512]{2,1,0:T(8,128)(2,1)} %values_ref.1) | copy-start | bytes 12582916
  0.8 14.5 %copy-start.3 = (bf16[32,1024]{1,0:T(8,128)(2,1)S(1)}, bf16[32,1024]{1,0:T(8,128)(2,1)}, u32[]{:S(2)}) copy-start(bf16[32,1024]{1,0:T(8,128)(2,1)} %value_up_ref.1) | copy-start | bytes 196612
  0.9 14.5 %copy-start.4 = (bf16[2,512]{1,0:T(2,128)(2,1)S(1)}, bf16[2,512]{1,0:T(2,128)(2,1)}, u32[]{:S(2)}) copy-start(bf16[2,512]{1,0:T(2,128)(2,1)} %new_keys_ref.1) | copy-start | bytes 6148
  0.9 14.5 %copy-start.5 = (bf16[2,512]{1,0:T(2,128)(2,1)S(1)}, bf16[2,512]{1,0:T(2,128)(2,1)}, u32[]{:S(2)}) copy-start(bf16[2,512]{1,0:T(2,128)(2,1)} %new_values_ref.1) | copy-start | bytes 6148
  0.9 14.5 %copy-start.6 = (s32[2]{0:T(128)S(1)}, s32[2]{0:T(128)}, u32[]{:S(2)}) copy-start(s32[2]{0:T(128)} %lengths_ref.1) | copy-start | bytes 28
  15.4 21.7 %copy-start.2 = (bf16[512,1024]{1,0:T(8,128)(2,1)S(1)}, bf16[512,1024]{1,0:T(8,128)(2,1)}, u32[]{:S(2)}) copy-start(bf16[512,1024]{1,0:T(8,128)(2,1)} %weight_ref.1) | copy-start | bytes 3145732

commit v4 on v3

--- a/solution.py
+++ b/solution.py
@@ -12,7 +12,7 @@
 VMEM = pltpu.VMEM
 MIB = 1024 * 1024
 LEAD, LATENT = 2 * 10**10, 2 * 10**10
-FIRST = (10, 10, 5, 10)
+FIRST = (14, 10, 5, 10)
 
 
 def iota(shape, dim):

time: 48.5 us -> 48.2 us (level)
  no operation moved by 1% of the time
where the time goes in v4:
time: 48.2 us; the launch traced here: 48 us
  blocking collectives  42.6 us (88%)
  Pallas kernels  4.45 us (9%)
  local copies, waits for them, and re-layouts  0.87 us (2%)
    all_to_all x4, blocking collectives, exchange(): lax.all_to_all(value, axis, 0, 0, axis_index_groups=[order], tiled=True)  42.6 us
    pallas_call x1, Pallas kernels, body(): call(functools.partial(attend_kernel, scale), [((peers, 72, 128), bf16)],...  2.81 us

profile of v4, /device:TPU:0, one launch (start us, length us, event | category | flops | bytes accessed | tf_op | source)
XLA Modules:
  0.0 48.0 jit_solution(11485465464120379516)
XLA Ops:
  0.0 0.0 copy-start.7
  0.0 0.0 copy-start.8
  0.0 0.8 %copy-done.7 = bf16[32,1024]{1,0:T(8,128)(2,1)S(1)} copy-done((bf16[32,1024]{1,0:T(8,128)(2,1)S(1)}, bf16[32,1024]{1,0:T(8,128)(2,1)}, u32[]{:S(2)}) %copy-start.7) | copy-done | bytes 65560
  0.8 0.0 copy-done.8
  0.9 0.0 copy-start.4
  0.9 0.0 copy-start.5
  0.9 0.0 copy-start.6
  0.9 0.3 latent.1
  1.2 14.3 %all_to_all.20.latent_ref = bf16[16,32,256]{2,1,0:T(8,128)(2,1)S(1)} all-to-all(bf16[16,32,256]{2,1,0:T(8,128)(2,1)S(1)} %latent.1), channel_id=1, replica_groups={{14,1,2,3,4,5,6,7,8,9,10,11,12,13,0,15},{30,17,18,19,20,21,22,23,24,25,..., dimensions={0} | all-to-all | bytes 524288 | tf_op jit(solution)/shard_map/all_to_all | solution.py:210
  15.5 0.0 copy-done
  15.5 0.0 copy-done.1
  15.5 0.0 copy-done.3
  15.5 0.0 copy-done.4
  15.5 0.0 copy-done.5
  15.5 0.0 copy-done.6
  15.5 0.0 copy-start.2
  15.6 2.8 %attend.1 = bf16[16,72,128]{2,1,0:T(8,128)(2,1)S(1)} custom-call(s32[2]{0:T(128)S(1)} %copy-done.6, bf16[16,32,256]{2,1,0:T(8,128)(2,1)S(1)} %all_to_all.20.latent_ref, bf16[2,2048,512]{2,1,0:T(8,128)(2,1)S(1)} %copy-done, bf16[2,2048,512]{2,1,0:T(8,128)(2,1)S(1)} %copy-done.1, bf16[2,512]{1,0:T(2,128)(2,1)S(1)} %copy-done.4, bf16[2,512]{1,0:T(2,128)(2,1)S(1)} %copy-done.5, ...), custom_call_target="tpu_custom_call" | custom-call | flops 1000000000 | tf_op jit(solution)/shard_map/attend/pallas_call | solution.py:227
  18.4 11.0 %all_to_all.21.parts_ref = bf16[16,72,128]{2,1,0:T(8,128)(2,1)S(1)} all-to-all(bf16[16,72,128]{2,1,0:T(8,128)(2,1)S(1)} %attend.1), channel_id=1, replica_groups={{10,1,2,3,4,5,6,7,8,9,0,11,12,13,14,15},{26,17,18,19,20,21,22,23,24,25,..., dimensions={0} | all-to-all | bytes 589824 | tf_op jit(solution)/shard_map/all_to_all | solution.py:210
  29.4 0.3 merge.1
  29.7 7.3 %all_to_all.22.attended_ref = bf16[8,8,128]{2,1,0:T(8,128)(2,1)S(1)} all-to-all(bf16[8,8,128]{2,1,0:T(8,128)(2,1)S(1)} %merge.1), channel_id=1, replica_groups={{80,16,32,48,64,0,96,112},{81,17,33,49,65,1,97,113},{82,18,34,50,66,2,9..., dimensions={0} | all-to-all | bytes 32768 | tf_op jit(solution)/shard_map/all_to_all | solution.py:210
  37.1 0.0 copy-done.2
  37.1 0.4 project.1
  37.4 9.9 %all_to_all.23.parts_ref = f32[16,8,128]{2,1,0:T(8,128)S(1)} all-to-all(f32[16,8,128]{2,1,0:T(8,128)S(1)} %project.1), channel_id=1, replica_groups={{10,1,2,3,4,5,6,7,8,9,0,11,12,13,14,15},{26,17,18,19,20,21,22,23,24,25,..., dimensions={0} | all-to-all | bytes 131072 | tf_op jit(solution)/shard_map/all_to_all | solution.py:210
  47.4 0.6 %total.1 = bf16[1,1024]{1,0:T(2,128)(2,1)} custom-call(f32[16,8,128]{2,1,0:T(8,128)S(1)} %all_to_all.23.parts_ref), custom_call_target="tpu_custom_call" | custom-call | tf_op jit(solution)/shard_map/total/pallas_call | solution.py:244
  (4 shorter events, 0.0 us)
Async XLA Ops:
  0.0 0.8 %copy-start.7 = (bf16[32,1024]{1,0:T(8,128)(2,1)S(1)}, bf16[32,1024]{1,0:T(8,128)(2,1)}, u32[]{:S(2)}) copy-start(bf16[32,1024]{1,0:T(8,128)(2,1)} %key_up_ref.1) | copy-start | bytes 196612
  0.0 0.8 %copy-start.8 = (bf16[2,64,128]{2,1,0:T(8,128)(2,1)S(1)}, bf16[2,64,128]{2,1,0:T(8,128)(2,1)}, u32[]{:S(2)}) copy-start(bf16[2,64,128]{2,1,0:T(8,128)(2,1)} %query_ref.1) | copy-start | bytes 98308
  0.8 14.7 %copy-start = (bf16[2,2048,512]{2,1,0:T(8,128)(2,1)S(1)}, bf16[2,2048,512]{2,1,0:T(8,128)(2,1)}, u32[]{:S(2)}) copy-start(bf16[2,2048,512]{2,1,0:T(8,128)(2,1)} %keys_ref.1) | copy-start | bytes 12582916
  0.8 14.7 %copy-start.1 = (bf16[2,2048,512]{2,1,0:T(8,128)(2,1)S(1)}, bf16[2,2048,512]{2,1,0:T(8,128)(2,1)}, u32[]{:S(2)}) copy-start(bf16[2,2048,512]{2,1,0:T(8,128)(2,1)} %values_ref.1) | copy-start | bytes 12582916
  0.8 14.7 %copy-start.3 = (bf16[32,1024]{1,0:T(8,128)(2,1)S(1)}, bf16[32,1024]{1,0:T(8,128)(2,1)}, u32[]{:S(2)}) copy-start(bf16[32,1024]{1,0:T(8,128)(2,1)} %value_up_ref.1) | copy-start | bytes 196612
  0.9 14.7 %copy-start.4 = (bf16[2,512]{1,0:T(2,128)(2,1)S(1)}, bf16[2,512]{1,0:T(2,128)(2,1)}, u32[]{:S(2)}) copy-start(bf16[2,512]{1,0:T(2,128)(2,1)} %new_keys_ref.1) | copy-start | bytes 6148
  0.9 14.7 %copy-start.5 = (bf16[2,512]{1,0:T(2,128)(2,1)S(1)}, bf16[2,512]{1,0:T(2,128)(2,1)}, u32[]{:S(2)}) copy-start(bf16[2,512]{1,0:T(2,128)(2,1)} %new_values_ref.1) | copy-start | bytes 6148
  0.9 14.7 %copy-start.6 = (s32[2]{0:T(128)S(1)}, s32[2]{0:T(128)}, u32[]{:S(2)}) copy-start(s32[2]{0:T(128)} %lengths_ref.1) | copy-start | bytes 28
  15.5 21.5 %copy-start.2 = (bf16[512,1024]{1,0:T(8,128)(2,1)S(1)}, bf16[512,1024]{1,0:T(8,128)(2,1)}, u32[]{:S(2)}) copy-start(bf16[512,1024]{1,0:T(8,128)(2,1)} %weight_ref.1) | copy-start | bytes 3145732

commit v5 on v4

--- a/solution.py
+++ b/solution.py
@@ -79,47 +79,53 @@
     ]
     second = ((iota((1, 128), 1) >> 2) & 1) == 1
     limit = jnp.where(second, lengths_ref[1], lengths_ref[0]) - shift
-    top = jnp.full((8, 128), FLOOR, jnp.float32)
-    for c in range(length // chunk):
-        at = pl.ds(c * chunk, chunk)
-        raw = jnp.dot(keys_ref[0, at, :], maps[0], preferred_element_type=jnp.float32)
-        raw += jnp.dot(keys_ref[1, at, :], maps[1], preferred_element_type=jnp.float32)
-        scores = (raw[:, :128] + raw[:, 128:]) * scale
-        live = iota((chunk, 128), 0) + c * chunk < limit
-        scores = jnp.where(live, scores, NEGATIVE)
-        scores_ref[at, :] = scores
-        top = jnp.maximum(top, jnp.max(scores.reshape(chunk // 8, 8, 128), axis=0))
+    half = length // 2
+    upper = ((iota((128, rank), 0) >> 2) & 1) == 1
+    tops, totals, summed = [], [], []
+    for h in range(2):
+        top = jnp.full((8, 128), FLOOR, jnp.float32)
+        for c in range(h * half, h * half + half, chunk):
+            at = pl.ds(c, chunk)
+            raw = jnp.dot(keys_ref[0, at, :], maps[0], preferred_element_type=jnp.float32)
+            raw += jnp.dot(keys_ref[1, at, :], maps[1], preferred_element_type=jnp.float32)
+            scores = (raw[:, :128] + raw[:, 128:]) * scale
+            scores = jnp.where(iota((chunk, 128), 0) + c < limit, scores, NEGATIVE)
+            scores_ref[at, :] = scores
+            top = jnp.maximum(top, jnp.max(scores.reshape(chunk // 8, 8, 128), axis=0))
+        tops.append(jnp.max(top, axis=0, keepdims=True))
     fresh = jnp.dot(new_keys_ref[...], maps[0], preferred_element_type=jnp.float32)[0:1]
     fresh += jnp.dot(new_keys_ref[...], maps[1], preferred_element_type=jnp.float32)[1:2]
     fresh = (fresh[:, :128] + fresh[:, 128:]) * scale
     fresh = jnp.where(shift == 0, fresh, NEGATIVE)
-    top = jnp.maximum(jnp.max(top, axis=0, keepdims=True), fresh)
-    total = jnp.zeros((8, 128), jnp.float32)
-    for c in range(length // chunk):
-        at = pl.ds(c * chunk, chunk)
-        weights = jnp.exp(scores_ref[at, :] - top)
-        total += jnp.sum(weights.reshape(chunk // 8, 8, 128), axis=0)
-        weights_ref[:, at] = weights.T.astype(jnp.bfloat16)
+    for h in range(2):
+        total = jnp.zeros((8, 128), jnp.float32)
+        for c in range(h * half, h * half + half, chunk):
+            at = pl.ds(c, chunk)
+            weights = jnp.exp(scores_ref[at, :] - tops[h])
+            total += jnp.sum(weights.reshape(chunk // 8, 8, 128), axis=0)
+            weights_ref[:, at] = weights.astype(jnp.bfloat16).T
+        totals.append(jnp.sum(total, axis=0, keepdims=True))
+        at = pl.ds(h * half, half)
+        sums = [
+            jnp.dot(weights_ref[:, at], values_ref[b, at, :], preferred_element_type=jnp.float32)
+            for b in range(2)
+        ]
+        summed.append(jnp.where(upper, sums[1], sums[0]))
+    top = jnp.maximum(jnp.maximum(tops[0], tops[1]), fresh)
+    factors = [jnp.exp(t - top) for t in tops]
     own = jnp.exp(fresh - top)
-    total = jnp.sum(total, axis=0, keepdims=True) + own
+    total = totals[0] * factors[0] + totals[1] * factors[1] + own
     top_high, rest = split(top)
     top_mid, top_low = split(rest)
     total_high, total_low = split(total)
     row = iota((128, 128), 0)
     table = jnp.zeros((128, 128), jnp.float32)
-    for k, line in enumerate((top_high, top_mid, top_low, total_high, total_low, own)):
+    for k, line in enumerate((top_high, top_mid, top_low, total_high, total_low, own, *factors)):
         table = jnp.where(row == k, line, table)
     table = table.T
-    own_column = table[:, 5:6]
-    sums = [
-        jnp.dot(weights_ref[...], values_ref[b], preferred_element_type=jnp.float32)
-        for b in range(2)
-    ]
     fresh_values = new_values_ref[...].astype(jnp.float32)
-    upper = ((iota((128, rank), 0) >> 2) & 1) == 1
-    summed = jnp.where(upper, sums[1], sums[0]) + own_column * jnp.where(
-        upper, fresh_values[1:2], fresh_values[0:1]
-    )
+    summed = summed[0] * table[:, 6:7] + summed[1] * table[:, 7:8]
+    summed += table[:, 5:6] * jnp.where(upper, fresh_values[1:2], fresh_values[0:1])
     for k in range(peers):
         lines = summed[8 * k : 8 * k + 8]
         stack = [lines[:, 128 * g : 128 * g + 128] for g in range(rank // 128)]

time: 48.2 us -> 48 us (level)
  no operation moved by 1% of the time
where the time goes in v5:
time: 48 us; the launch traced here: 47.8 us
  blocking collectives  42.6 us (89%)
  Pallas kernels  4.25 us (9%)
  local copies, waits for them, and re-layouts  0.87 us (2%)
    all_to_all x4, blocking collectives, exchange(): lax.all_to_all(value, axis, 0, 0, axis_index_groups=[order], tiled=True)  42.6 us
    pallas_call x1, Pallas kernels, body(): call(functools.partial(attend_kernel, scale), [((peers, 72, 128), bf16)],...  2.61 us

profile of v5, /device:TPU:0, one launch (start us, length us, event | category | flops | bytes accessed | tf_op | source)
XLA Modules:
  0.0 47.8 jit_solution(9891446049486911755)
XLA Ops:
  0.0 0.0 copy-start.7
  0.0 0.0 copy-start.8
  0.0 0.8 %copy-done.7 = bf16[32,1024]{1,0:T(8,128)(2,1)S(1)} copy-done((bf16[32,1024]{1,0:T(8,128)(2,1)S(1)}, bf16[32,1024]{1,0:T(8,128)(2,1)}, u32[]{:S(2)}) %copy-start.7) | copy-done | bytes 65560
  0.8 0.0 copy-done.8
  0.9 0.0 copy-start.4
  0.9 0.0 copy-start.5
  0.9 0.0 copy-start.6
  0.9 0.3 latent.1
  1.2 14.3 %all_to_all.20.latent_ref = bf16[16,32,256]{2,1,0:T(8,128)(2,1)S(1)} all-to-all(bf16[16,32,256]{2,1,0:T(8,128)(2,1)S(1)} %latent.1), channel_id=1, replica_groups={{14,1,2,3,4,5,6,7,8,9,10,11,12,13,0,15},{30,17,18,19,20,21,22,23,24,25,..., dimensions={0} | all-to-all | bytes 524288 | tf_op jit(solution)/shard_map/all_to_all | solution.py:216
  15.5 0.0 copy-done
  15.5 0.0 copy-done.1
  15.5 0.0 copy-done.3
  15.5 0.0 copy-done.4
  15.5 0.0 copy-done.5
  15.5 0.0 copy-done.6
  15.5 0.0 copy-start.2
  15.6 2.6 %attend.1 = bf16[16,72,128]{2,1,0:T(8,128)(2,1)S(1)} custom-call(s32[2]{0:T(128)S(1)} %copy-done.6, bf16[16,32,256]{2,1,0:T(8,128)(2,1)S(1)} %all_to_all.20.latent_ref, bf16[2,2048,512]{2,1,0:T(8,128)(2,1)S(1)} %copy-done, bf16[2,2048,512]{2,1,0:T(8,128)(2,1)S(1)} %copy-done.1, bf16[2,512]{1,0:T(2,128)(2,1)S(1)} %copy-done.4, bf16[2,512]{1,0:T(2,128)(2,1)S(1)} %copy-done.5, ...), custom_call_target="tpu_custom_call" | custom-call | flops 1000000000 | tf_op jit(solution)/shard_map/attend/pallas_call | solution.py:233
  18.2 11.0 %all_to_all.21.parts_ref = bf16[16,72,128]{2,1,0:T(8,128)(2,1)S(1)} all-to-all(bf16[16,72,128]{2,1,0:T(8,128)(2,1)S(1)} %attend.1), channel_id=1, replica_groups={{10,1,2,3,4,5,6,7,8,9,0,11,12,13,14,15},{26,17,18,19,20,21,22,23,24,25,..., dimensions={0} | all-to-all | bytes 589824 | tf_op jit(solution)/shard_map/all_to_all | solution.py:216
  29.2 0.3 merge.1
  29.5 7.3 %all_to_all.22.attended_ref = bf16[8,8,128]{2,1,0:T(8,128)(2,1)S(1)} all-to-all(bf16[8,8,128]{2,1,0:T(8,128)(2,1)S(1)} %merge.1), channel_id=1, replica_groups={{80,16,32,48,64,0,96,112},{81,17,33,49,65,1,97,113},{82,18,34,50,66,2,9..., dimensions={0} | all-to-all | bytes 32768 | tf_op jit(solution)/shard_map/all_to_all | solution.py:216
  36.8 0.0 copy-done.2
  36.8 0.4 project.1
  37.2 10.0 %all_to_all.23.parts_ref = f32[16,8,128]{2,1,0:T(8,128)S(1)} all-to-all(f32[16,8,128]{2,1,0:T(8,128)S(1)} %project.1), channel_id=1, replica_groups={{10,1,2,3,4,5,6,7,8,9,0,11,12,13,14,15},{26,17,18,19,20,21,22,23,24,25,..., dimensions={0} | all-to-all | bytes 131072 | tf_op jit(solution)/shard_map/all_to_all | solution.py:216
  47.2 0.6 %total.1 = bf16[1,1024]{1,0:T(2,128)(2,1)} custom-call(f32[16,8,128]{2,1,0:T(8,128)S(1)} %all_to_all.23.parts_ref), custom_call_target="tpu_custom_call" | custom-call | tf_op jit(solution)/shard_map/total/pallas_call | solution.py:250
  (4 shorter events, 0.0 us)
Async XLA Ops:
  0.0 0.8 %copy-start.7 = (bf16[32,1024]{1,0:T(8,128)(2,1)S(1)}, bf16[32,1024]{1,0:T(8,128)(2,1)}, u32[]{:S(2)}) copy-start(bf16[32,1024]{1,0:T(8,128)(2,1)} %key_up_ref.1) | copy-start | bytes 196612
  0.0 0.8 %copy-start.8 = (bf16[2,64,128]{2,1,0:T(8,128)(2,1)S(1)}, bf16[2,64,128]{2,1,0:T(8,128)(2,1)}, u32[]{:S(2)}) copy-start(bf16[2,64,128]{2,1,0:T(8,128)(2,1)} %query_ref.1) | copy-start | bytes 98308
  0.8 14.7 %copy-start = (bf16[2,2048,512]{2,1,0:T(8,128)(2,1)S(1)}, bf16[2,2048,512]{2,1,0:T(8,128)(2,1)}, u32[]{:S(2)}) copy-start(bf16[2,2048,512]{2,1,0:T(8,128)(2,1)} %keys_ref.1) | copy-start | bytes 12582916
  0.8 14.7 %copy-start.1 = (bf16[2,2048,512]{2,1,0:T(8,128)(2,1)S(1)}, bf16[2,2048,512]{2,1,0:T(8,128)(2,1)}, u32[]{:S(2)}) copy-start(bf16[2,2048,512]{2,1,0:T(8,128)(2,1)} %values_ref.1) | copy-start | bytes 12582916
  0.8 14.7 %copy-start.3 = (bf16[32,1024]{1,0:T(8,128)(2,1)S(1)}, bf16[32,1024]{1,0:T(8,128)(2,1)}, u32[]{:S(2)}) copy-start(bf16[32,1024]{1,0:T(8,128)(2,1)} %value_up_ref.1) | copy-start | bytes 196612
  0.9 14.7 %copy-start.4 = (bf16[2,512]{1,0:T(2,128)(2,1)S(1)}, bf16[2,512]{1,0:T(2,128)(2,1)}, u32[]{:S(2)}) copy-start(bf16[2,512]{1,0:T(2,128)(2,1)} %new_keys_ref.1) | copy-start | bytes 6148
  0.9 14.7 %copy-start.5 = (bf16[2,512]{1,0:T(2,128)(2,1)S(1)}, bf16[2,512]{1,0:T(2,128)(2,1)}, u32[]{:S(2)}) copy-start(bf16[2,512]{1,0:T(2,128)(2,1)} %new_values_ref.1) | copy-start | bytes 6148
  0.9 14.7 %copy-start.6 = (s32[2]{0:T(128)S(1)}, s32[2]{0:T(128)}, u32[]{:S(2)}) copy-start(s32[2]{0:T(128)} %lengths_ref.1) | copy-start | bytes 28
  15.5 21.3 %copy-start.2 = (bf16[512,1024]{1,0:T(8,128)(2,1)S(1)}, bf16[512,1024]{1,0:T(8,128)(2,1)}, u32[]{:S(2)}) copy-start(bf16[512,1024]{1,0:T(8,128)(2,1)} %weight_ref.1) | copy-start | bytes 3145732
